TPU v7x, 32 devices: a whole 2x2x4 slice. The times are simulated.
32 devices in a mesh: lon: 4 (over z), lat: 4 (over x, core), mem: 2 (over y).
Axes of the slice: x: 2, y: 2, z: 4, core: 2. Of those that a mesh axis runs over, the one named last changes fastest.
Arguments:
- tokens: bfloat16 [4, 8, 136, 24, 192], P('mem', None, 'lat', 'lon'), parts along dimension 0, may hold values from -6 to 6
- band_rows: int32 [4, 2], P('lat'), may hold values from 0 to 89, as said below
- down_gain: float32 [768], replicated, may hold values from 0.1 to 1.9
- down_shift: float32 [768], replicated, may hold values from -3 to 3
- down_weight: bfloat16 [768, 384], P(('lon', 'lat')), may hold values from -0.21875 to 0.21875
- up_weight: bfloat16 [384, 768], P(('lon', 'lat')), may hold values from -0.3125 to 0.3125
- up_gain: float32 [192], replicated, may hold values from 0.1 to 1.9
- up_shift: float32 [192], replicated, may hold values from -3 to 3
- mix_weight: bfloat16 [192, 192], replicated, may hold values from -0.4375 to 0.4375
Outputs:
- expanded: bfloat16 [4, 8, 136, 24, 192], P('mem', None, 'lat', 'lon'), parts along dimension 0
There are 2 independent parts, one for each index of `mem`. A program takes and returns all parts, laid end to end along the dimension named above; an argument that names none is the same for every part. Nothing has to cross between parts.
Inputs may be any that keep to these rules, and one draw needn't show every extreme that they name: `band_rows`: row b holds band b's first latitude row and one past its last; the bands cover rows 0 to 88 in order without gaps; band 0 holds an odd number of rows and every other band an even number; each band holds at least 2 * (5) rows and at most 34, and some band other than band 0 holds exactly 34.
All inputs are finite; a program needn't handle non-finite values.
Results may differ from a plain program's by a relative error of at most 0.0062.
Values may be sent and summed in bfloat16 or wider, within the bound.
A program may use at most 64 MiB of HBM per device.

v0:
```python
import jax
import jax.numpy as jnp
from jax import lax
from jax.sharding import PartitionSpec as P


def shifted(block, axis, distance):
    devices = range(lax.axis_size(axis))
    route = [((i - distance) % len(devices), i) for i in devices]
    return lax.ppermute(block, axis, route)


def passed_along(block, axis, distance):
    devices = range(lax.axis_size(axis))
    route = [(i - distance, i) for i in devices if i - distance in devices]
    return lax.ppermute(block, axis, route)


def normalize(values, scale_gain, bias_shift):
    average = jnp.mean(values, axis=-1, keepdims=True)
    centred = values - average
    spread = jnp.mean(centred * centred, axis=-1, keepdims=True)
    return centred * lax.rsqrt(spread + 1e-05) * scale_gain + bias_shift


def body(
    tokens, band_rows, down_gain, down_shift, down_weight, up_weight, up_gain, up_shift, mix_weight
):
    members, levels, slot_count, columns, features = tokens.shape
    half_rows = slot_count // 2 + 1
    first_row = band_rows[0, 0]
    live_rows = band_rows[0, 1] - first_row
    lat_odd = first_row % 2
    row_ids = lax.broadcasted_iota(jnp.int32, (1, 1, slot_count, 1, 1), 2)
    fields = jnp.where(row_ids < live_rows, tokens, jnp.zeros_like(tokens))
    right_col = shifted(fields[:, :, :, :1], "lon", -1)
    window = jnp.concatenate([fields[:, :, :, 1:], right_col], axis=3)
    window_cols = window.shape[3]
    half_cols = window_cols // 2
    next_first = passed_along(window[:, :, :1], "lat", -1)
    zero_rows = jnp.zeros((members, levels, 2, window_cols, features), window.dtype)
    extended = jnp.concatenate([window, zero_rows, zero_rows[:, :, :1]], axis=2)
    ext_ids = lax.broadcasted_iota(jnp.int32, (1, 1, slot_count + 3, 1, 1), 2)
    extended = jnp.where(ext_ids == live_rows, next_first, extended)
    patch_rows = lax.dynamic_slice_in_dim(extended, lat_odd, 2 * half_rows, 2)
    merged = patch_rows.reshape(members, levels, half_rows, 2, half_cols, 2, features)
    merged = merged.transpose(0, 1, 2, 4, 5, 3, 6).reshape(
        members * levels * half_rows * half_cols, 4 * features
    )
    merged_norm = normalize(merged.astype(jnp.float32), down_gain, down_shift).astype(jnp.bfloat16)
    columns_used = merged_norm
    coarse = jnp.dot(
        columns_used,
        lax.all_gather(down_weight, ("lon", "lat"), axis=0, tiled=True),
        preferred_element_type=jnp.float32,
    )
    coarse = coarse.astype(jnp.bfloat16)
    columns_used = coarse
    grown = jnp.dot(
        columns_used,
        lax.all_gather(up_weight, ("lon", "lat"), axis=0, tiled=True),
        preferred_element_type=jnp.float32,
    )
    grown = grown.reshape(members, levels, half_rows, half_cols, 2, 2, features)
    grown = grown.transpose(0, 1, 2, 4, 3, 5, 6).reshape(
        members, levels, 2 * half_rows, window_cols, features
    )
    fine_norm = normalize(grown, up_gain, up_shift).astype(jnp.bfloat16)
    fine_out = jnp.dot(
        fine_norm.reshape(-1, features), mix_weight, preferred_element_type=jnp.float32
    )
    fine_out = fine_out.astype(jnp.bfloat16).reshape(
        members, levels, 2 * half_rows, window_cols, features
    )
    overflow_row = lax.dynamic_slice_in_dim(fine_out, live_rows - lat_odd, 1, 2)
    from_above = passed_along(overflow_row, "lat", 1)
    padded_rows = jnp.concatenate([jnp.zeros_like(overflow_row), fine_out], axis=2)
    owned = lax.dynamic_slice_in_dim(padded_rows, 1 - lat_odd, slot_count, 2)
    owned = jnp.where((row_ids == 0) & (lat_odd == 1), from_above, owned)
    overflow_col = owned[:, :, :, columns - 1 :]
    from_left = shifted(overflow_col, "lon", 1)
    owned = jnp.concatenate([from_left, owned[:, :, :, : columns - 1]], axis=3)
    return jnp.where(row_ids < live_rows, owned, jnp.zeros_like(owned))


def solution(mesh):
    return jax.shard_map(
        body,
        mesh=mesh,
        in_specs=(
            P("mem", None, "lat", "lon", None),
            P("lat", None),
            P(),
            P(),
            P(("lon", "lat"), None),
            P(("lon", "lat"), None),
            P(),
            P(),
            P(),
        ),
        out_specs=P("mem", None, "lat", "lon", None),
        check_vma=False,
    )
```

profile of v0, /device:TPU:0, one launch (start us, length us, event | category | flops | bytes accessed | tf_op | source)
XLA Modules:
  0.0 134.9 jit_solution(14760807719825916473)
XLA Ops:
  0.0 1.3 fusion.16
  2.6 1.6 %broadcast_select_fusion = bf16[2,8,34,6,192]{4,1,3,2,0:T(8,128)(2,1)S(1)} fusion(bf16[2,8,34,6,192]{4,1,3,2,0:T(8,128)(2,1)} %param.9, pred[34]{0:T(512)(128)(4,1)S(1)} %iota_compare_fusion.1), kind=kLoop, calls=%fused_computation.21 | loop fusion | flops 626688 | bytes 2506786 | tf_op jit(solution)/shard_map/jit(_where)/select_n | solution.py:35
  5.0 5.1 %collective-permute-start = (bf16[2,8,34,1,192]{4,1,3,2,0:T(8,128)(2,1)}, bf16[2,8,34,1,192]{4,1,3,2,0:T(8,128)(2,1)S(1)}, u32[]{:S(2)}, u32[]{:S(2)}) collective-permute-start(bf16[2,8,34,1,192]{4,1,3,2,0:T(8,128)(2,1)} %slice.29), channel_id=1, source_target_pairs={{8,0},{16,8},{24,16},{0,24},{9,1},{17,9},{25,17},{1,25},{10,2},{18... | collective-permute-start | bytes 626696 | tf_op jit(solution)/shard_map/ppermute | solution.py:10
  12.0 22.9 %all_gather.6 = bf16[768,384]{1,0:T(8,128)(2,1)} all-gather(bf16[48,384]{1,0:T(8,128)(2,1)S(1)} %copy-done.4), channel_id=1, replica_groups=mesh['lon'=4,'lat'=4,'mem'=2] {'lon','lat'}, dimensions={0}, use_global_device_ids=true | all-gather | bytes 626688 | tf_op jit(solution)/shard_map/all_gather | solution.py:54
  35.0 20.4 %all_gather.7 = bf16[384,768]{1,0:T(8,128)(2,1)} all-gather(bf16[24,768]{1,0:T(8,128)(2,1)S(1)} %copy-done.5), channel_id=1, replica_groups=mesh['lon'=4,'lat'=4,'mem'=2] {'lon','lat'}, dimensions={0}, use_global_device_ids=true | all-gather | bytes 626688 | tf_op jit(solution)/shard_map/all_gather | solution.py:61
  55.4 1.3 collective-permute-start.1
  57.0 1.5 %collective-permute-done.1 = bf16[2,8,1,6,192]{4,1,3,2,0:T(8,128)(2,1)S(1)} collective-permute-done((bf16[2,8,1,6,192]{4,1,3,2,0:T(8,128)(2,1)S(1)}, bf16[2,8,1,6,192]{4,1,3,2,0:T(8,128)(2,1)S(1)}, u32[]{:S(2)}, u32[]{:S(2)}) %collective-permute-start.1) | collective-permute-done | bytes 36896 | tf_op jit(solution)/shard_map/ppermute | solution.py:16
  59.2 1.4 %fusion.3 = bf16[2,8,36,6,192]{4,1,3,2,0:T(8,128)(2,1)S(1)} fusion(s32[]{:T(128)S(6)} %select_n.34, bf16[2,8,34,5,192]{4,1,3,2,0:T(8,128)(2,1)S(1)} %slice.28, bf16[2,8,34,1,192]{4,1,3,2,0:T(8,128)(2,1)S(1)} %collective-permute-done, pred[36]{0:T(512)(128)(4,1)S(1)} %dynamic-slice.2, bf16[2,8,6,192]{3,1,2,0:T(8,128)(2,1)} %bitcast.30, ...), kind=kLoop, calls=%fused_computation.13 | loop fusion | flops 2654208 | bytes 2617528 | tf_op jit(solution)/shard_map/jit(_where)/select_n | solution.py:44
  61.4 2.3 %convert_bitcast_fusion = f32[2,8,18,3,2,2,192]{6,1,4,3,5,2,0:T(8,128)} fusion(bf16[2,8,18,2,3,2,192]{6,1,5,4,3,2,0:T(8,128)(2,1)S(1)} %bitcast.26), kind=kLoop, calls=%fused_computation.1 | loop fusion | flops 663552 | bytes 3981312 | tf_op jit(solution)/shard_map/convert_element_type | solution.py:50
  65.1 6.5 %copy.32 = f32[2,8,18,3,2,2,192]{6,5,4,3,2,1,0:T(2,128)} copy(f32[2,8,18,3,2,2,192]{6,1,4,3,5,2,0:T(8,128)} %convert_bitcast_fusion) | data formatting | bytes 5308416 | tf_op jit(solution)/shard_map/convert_element_type | solution.py:50
  71.7 4.8 %reshape.108 = f32[864,768]{1,0:T(8,128)S(1)} reshape(f32[2,8,18,3,2,2,192]{6,5,4,3,2,1,0:T(2,128)} %copy.32) | data formatting | bytes 5308416 | tf_op jit(solution)/shard_map/convert_element_type | solution.py:50
  76.5 4.4 %fusion.14 = f32[864,768]{1,0:T(8,128)} fusion(bf16[384,768]{1,0:T(8,128)(2,1)} %all_gather.7, bf16[768,384]{1,0:T(8,128)(2,1)S(1)} %copy-done.2, f32[864,768]{1,0:T(8,128)S(1)} %reshape.108, f32[768]{0:T(1024)S(1)} %copy-done.8, f32[768]{0:T(1024)S(1)} %copy-done.9, f32[864]{0:T(1024)S(1)} %rsqrt.23, f32[864]{0:T(1024)S(1)} %div.17), kind=kOutput, calls=%fused_computation.27 | convolution fusion | flops 1022865408 | bytes 6501120 | tf_op jit(solution)/shard_map/dot_general | solution.py:59
  80.9 6.3 %reshape.105 = f32[2,8,18,3,2,2,192]{6,5,4,3,2,1,0:T(2,128)} reshape(f32[864,768]{1,0:T(8,128)} %fusion.14) | data formatting | bytes 5308416 | tf_op jit(solution)/shard_map/reshape | solution.py:64
  87.2 4.2 %fusion.15 = f32[2,8,18,2,3,2]{5,4,3,2,1,0:T(4,128)S(1)} fusion(f32[2,8,18,3,2,2,192]{6,5,4,3,2,1,0:T(2,128)} %reshape.105), kind=kLoop, calls=%fused_computation.39 | loop fusion | flops 660096 | bytes 2668032 | tf_op jit(solution)/shard_map/reduce_sum | solution.py:20
  92.4 5.9 %multiply_reduce_fusion = f32[2,8,18,2,3,2]{5,4,3,2,1,0:T(4,128)S(1)} fusion(f32[2,8,18,2,3,2]{5,4,3,2,1,0:T(4,128)S(1)} %broadcast_multiply_fusion, f32[2,8,18,3,2,2,192]{6,5,4,3,2,1,0:T(2,128)} %reshape.105), kind=kLoop, calls=%fused_computation.4 | loop fusion | flops 1987200 | bytes 2681856 | tf_op jit(solution)/shard_map/reduce_sum | solution.py:22
  98.3 3.0 %copy.48 = f32[2,8,18,3,2,2,192]{6,5,3,4,2,1,0:T(2,128)} copy(f32[2,8,18,3,2,2,192]{6,5,4,3,2,1,0:T(2,128)S(1)} %copy-done.1) | data formatting | bytes 5308416 | tf_op jit(solution)/shard_map/reshape | solution.py:64
  101.3 5.4 %reshape.106 = f32[3456,192]{1,0:T(8,128)} reshape(f32[2,8,18,2,3,2,192]{6,5,4,3,2,1,0:T(2,128)} %bitcast.28) | data formatting | bytes 5308416 | tf_op jit(solution)/shard_map/reshape | solution.py:65
  107.7 3.3 %convolution_convert_fusion = bf16[3456,192]{0,1:T(8,128)(2,1)S(1)} fusion(bf16[192,192]{1,0:T(8,128)(2,1)S(1)} %copy-done, f32[3456,192]{1,0:T(8,128)} %reshape.106, f32[192]{0:T(256)S(1)} %copy-done.6, f32[192]{0:T(256)S(1)} %copy-done.7, f32[3456]{0:T(1024)S(1)} %rsqrt.25, f32[3456]{0:T(1024)S(1)} %div.20), kind=kOutput, calls=%fused_computation | convolution fusion | flops 258785280 | bytes 4084224 | tf_op jit(solution)/shard_map/dot_general | solution.py:69
  111.0 2.2 %copy.39 = bf16[3456,192]{1,0:T(8,128)(2,1)} copy(bf16[3456,192]{0,1:T(8,128)(2,1)S(1)} %convolution_convert_fusion) | data formatting | bytes 2654208 | tf_op jit(solution)/shard_map/convert_element_type | solution.py:72
  113.2 2.8 %reshape.107 = bf16[2,8,36,6,192]{4,3,2,1,0:T(8,128)(2,1)S(1)} reshape(bf16[3456,192]{1,0:T(8,128)(2,1)} %copy.39) | data formatting | bytes 2654208 | tf_op jit(solution)/shard_map/reshape | solution.py:72
  116.1 4.5 %collective-permute-start.2 = (bf16[2,8,1,6,192]{4,3,2,1,0:T(8,128)(2,1)S(1)}, bf16[2,8,1,6,192]{4,3,2,1,0:T(8,128)(2,1)S(1)}, u32[]{:S(2)}, u32[]{:S(2)}) collective-permute-start(bf16[2,8,1,6,192]{4,3,2,1,0:T(8,128)(2,1)S(1)} %constant_dynamic-slice_fusion), channel_id=1, source_target_pairs={{0,2},{2,4},{4,6},{1,3},{3,5},{5,7},{8,10},{10,12},{12,14},{9,11},... | collective-permute-start | bytes 110600 | tf_op jit(solution)/shard_map/ppermute | solution.py:16
  120.6 1.9 %copy.41 = bf16[2,8,36,6,192]{4,1,3,2,0:T(8,128)(2,1)S(1)} copy(bf16[2,8,36,6,192]{4,3,2,1,0:T(8,128)(2,1)S(1)} %reshape.107) | data formatting | bytes 2654208 | tf_op jit(solution)/shard_map/reshape | solution.py:72
  123.1 10.3 %collective-permute-done.3 = bf16[2,8,34,1,192]{4,1,3,2,0:T(8,128)(2,1)S(1)} collective-permute-done((bf16[2,8,34,1,192]{4,1,3,2,0:T(8,128)(2,1)S(1)}, bf16[2,8,34,1,192]{4,1,3,2,0:T(8,128)(2,1)S(1)}, u32[]{:S(2)}, u32[]{:S(2)}) %collective-permute-start.3) | collective-permute-done | bytes 208928 | tf_op jit(solution)/shard_map/ppermute | solution.py:10
  133.3 1.5 %maximum_select_fusion = bf16[2,8,34,6,192]{4,1,3,2,0:T(8,128)(2,1)} fusion(bf16[2,8,34,5,192]{4,1,3,2,0:T(8,128)(2,1)S(1)} %slice.31, bf16[2,8,34,1,192]{4,1,3,2,0:T(8,128)(2,1)S(1)} %collective-permute-done.3, pred[34]{0:T(512)(128)(4,1)S(1)} %iota_compare_fusion.1), kind=kLoop, calls=%fused_computation.20 | loop fusion | flops 1253376 | bytes 2506786 | tf_op jit(solution)/shard_map/jit(_where)/select_n | solution.py:83
  (54 shorter events, 6.5 us)
Async XLA Ops:
  0.0 107.7 %copy-start = (bf16[192,192]{1,0:T(8,128)(2,1)S(1)}, bf16[192,192]{1,0:T(8,128)(2,1)}, u32[]{:S(2)}) copy-start(bf16[192,192]{1,0:T(8,128)(2,1)} %param.17) | copy-start | bytes 221188
  4.2 7.8 %copy-start.4 = (bf16[48,384]{1,0:T(8,128)(2,1)S(1)}, bf16[48,384]{1,0:T(8,128)(2,1)}, u32[]{:S(2)}) copy-start(bf16[48,384]{1,0:T(8,128)(2,1)} %param.13) | copy-start | bytes 110596
  5.0 30.0 %copy-start.5 = (bf16[24,768]{1,0:T(8,128)(2,1)S(1)}, bf16[24,768]{1,0:T(8,128)(2,1)}, u32[]{:S(2)}) copy-start(bf16[24,768]{1,0:T(8,128)(2,1)} %param.14) | copy-start | bytes 110596
  5.0 50.4 %collective-permute-start = (bf16[2,8,34,1,192]{4,1,3,2,0:T(8,128)(2,1)}, bf16[2,8,34,1,192]{4,1,3,2,0:T(8,128)(2,1)S(1)}, u32[]{:S(2)}, u32[]{:S(2)}) collective-permute-start(bf16[2,8,34,1,192]{4,1,3,2,0:T(8,128)(2,1)} %slice.29), channel_id=1, source_target_pairs={{8,0},{16,8},{24,16},{0,24},{9,1},{17,9},{25,17},{1,25},{10,2},{18... | collective-permute-start | bytes 626696 | tf_op jit(solution)/shard_map/ppermute | solution.py:10
  55.4 3.1 %collective-permute-start.1 = (bf16[2,8,1,6,192]{4,1,3,2,0:T(8,128)(2,1)S(1)}, bf16[2,8,1,6,192]{4,1,3,2,0:T(8,128)(2,1)S(1)}, u32[]{:S(2)}, u32[]{:S(2)}) collective-permute-start(bf16[2,8,1,6,192]{4,1,3,2,0:T(8,128)(2,1)S(1)} %pad_maximum_fusion), channel_id=1, source_target_pairs={{2,0},{4,2},{6,4},{3,1},{5,3},{7,5},{10,8},{12,10},{14,12},{11,9},... | collective-permute-start | bytes 110600 | tf_op jit(solution)/shard_map/ppermute | solution.py:16
  58.5 0.6 copy-start.3
  71.7 4.8 %copy-start.2 = (bf16[768,384]{1,0:T(8,128)(2,1)S(1)}, bf16[768,384]{1,0:T(8,128)(2,1)}, u32[]{:S(2)}) copy-start(bf16[768,384]{1,0:T(8,128)(2,1)} %all_gather.6) | copy-start | bytes 1769476
  71.7 4.9 %copy-start.8 = (f32[768]{0:T(1024)S(1)}, f32[768]{0:T(1024)}, u32[]{:S(2)}) copy-start(f32[768]{0:T(1024)} %param.12) | copy-start | bytes 9220
  71.7 4.9 %copy-start.9 = (f32[768]{0:T(1024)S(1)}, f32[768]{0:T(1024)}, u32[]{:S(2)}) copy-start(f32[768]{0:T(1024)} %param.11) | copy-start | bytes 9220
  92.4 5.9 %copy-start.1 = (f32[2,8,18,3,2,2,192]{6,5,4,3,2,1,0:T(2,128)S(1)}, f32[2,8,18,3,2,2,192]{6,5,4,3,2,1,0:T(2,128)}, u32[]{:S(2)}) copy-start(f32[2,8,18,3,2,2,192]{6,5,4,3,2,1,0:T(2,128)} %reshape.105) | copy-start | bytes 7962628
  106.7 1.0 copy-start.6
  106.7 1.0 copy-start.7
  116.1 6.5 %collective-permute-start.2 = (bf16[2,8,1,6,192]{4,3,2,1,0:T(8,128)(2,1)S(1)}, bf16[2,8,1,6,192]{4,3,2,1,0:T(8,128)(2,1)S(1)}, u32[]{:S(2)}, u32[]{:S(2)}) collective-permute-start(bf16[2,8,1,6,192]{4,3,2,1,0:T(8,128)(2,1)S(1)} %constant_dynamic-slice_fusion), channel_id=1, source_target_pairs={{0,2},{2,4},{4,6},{1,3},{3,5},{5,7},{8,10},{10,12},{12,14},{9,11},... | collective-permute-start | bytes 110600 | tf_op jit(solution)/shard_map/ppermute | solution.py:16
  122.9 10.4 %collective-permute-start.3 = (bf16[2,8,34,1,192]{4,1,3,2,0:T(8,128)(2,1)S(1)}, bf16[2,8,34,1,192]{4,1,3,2,0:T(8,128)(2,1)S(1)}, u32[]{:S(2)}, u32[]{:S(2)}) collective-permute-start(bf16[2,8,34,1,192]{4,1,3,2,0:T(8,128)(2,1)S(1)} %slice.30), channel_id=1, source_target_pairs={{24,0},{0,8},{8,16},{16,24},{25,1},{1,9},{9,17},{17,25},{26,2},{2,... | collective-permute-start | bytes 626696 | tf_op jit(solution)/shard_map/ppermute | solution.py:10
where the time goes:
time: 136 us; the launch traced here: 135 us
  blocking collectives  43.4 us (32%)
  local copies, waits for them, and re-layouts  38.6 us (28%)
  other arithmetic  19.2 us (14%)
  waiting for transfers between devices  11.8 us (9%)
  starting transfers between devices  11 us (8%)
  matrix products  7.64 us (6%)
  between operations  3.41 us (3%)
    all_gather x1, blocking collectives, body(): lax.all_gather(down_weight, ('lon', 'lat'), axis=0, tiled=True)  22.9 us
    all_gather x1, blocking collectives, body(): lax.all_gather(up_weight, ('lon', 'lat'), axis=0, tiled=True)  20.4 us
    convert_element_type x2, local copies, waits for them, and re-layouts, body(): merged.astype(jnp.float32)  11.4 us
    ppermute x2, waiting for transfers between devices, shifted(): return lax.ppermute(block, axis, route)  10.3 us
    reshape x2, local copies, waits for them, and re-layouts, body(): grown = grown.reshape(members, levels, half_rows, half_cols, 2, 2, features)  9.24 us
    reduce_sum x2, other arithmetic, normalize(): spread = jnp.mean(centred * centred, axis=-1, keepdims=True)  6.61 us
    ppermute x2, starting transfers between devices, passed_along(): return lax.ppermute(block, axis, route)  5.84 us
    reshape x1, local copies, waits for them, and re-layouts, body(): grown.transpose(0, 1, 2, 4, 3, 5, 6)  5.4 us
  transfers between devices with their start and end apart: 4, of which 2 were waited for; matrix products, arithmetic and copies ran while one was open for 2% of the time, Pallas kernels for 0%

commit v1 on v0

--- a/solution.py
+++ b/solution.py
@@ -51,7 +51,12 @@
     columns_used = merged_norm
     coarse = jnp.dot(
         columns_used,
-        lax.all_gather(down_weight, ("lon", "lat"), axis=0, tiled=True),
+        jnp.concatenate(
+            lax.all_to_all(
+                jnp.stack([down_weight] * lax.axis_size(("lon", "lat"))), ("lon", "lat"), 0, 0
+            ),
+            axis=0,
+        ),
         preferred_element_type=jnp.float32,
     )
     coarse = coarse.astype(jnp.bfloat16)

time: 136 us -> 109 us (0.80)
  blocking collectives: 43.4 us -> 27.2 us
  local copies, waits for them, and re-layouts: 38.6 us -> 28.3 us
  starting transfers between devices: 11 us -> 16.3 us
  other arithmetic: 19.2 us -> 15.5 us
    all_gather x1 -> x0, blocking collectives: 22.9 us -> none  [body(): lax.all_gather(down_weight, ('lon', 'lat'), axis=0, tiled=True)]
    convert_element_type x2, local copies, waits for them, and re-layouts: 11.4 us -> 3.66 us  [body(): normalize(merged.astype(jnp.float32), down_gain, down_shift)]
    all_gather x1, blocking collectives: 20.4 us -> 27.2 us  [body(): lax.all_gather(up_weight, ('lon', 'lat'), axis=0, tiled=True)]
    all_to_all x0 -> x1, starting transfers between devices: none -> 4.38 us  [body(): lax.all_to_all(jnp.stack([down_weight] * lax.axis_size(('lon', 'lat'))),...]
    reshape x2, local copies, waits for them, and re-layouts: 9.24 us -> 7.43 us  [body(): grown = grown.reshape(members, levels, half_rows, half_cols, 2, 2, features)]
    convert_element_type x1, other arithmetic: 2.27 us -> 0.71 us  [body(): normalize(merged.astype(jnp.float32), down_gain, down_shift)]
    reduce_sum x2, other arithmetic: 6.61 us -> 5.11 us  [normalize(): spread = jnp.mean(centred * centred, axis=-1, keepdims=True)]
  transfers between devices with their start and end apart: 4 -> 5, of which waited for: 2 -> 2; matrix products, arithmetic and copies ran while one was open for 2% -> 9% of each run, Pallas kernels for 0% -> 0%
where the time goes in v1:
time: 109 us; the launch traced here: 108 us
  local copies, waits for them, and re-layouts  28.3 us (26%)
  blocking collectives  27.2 us (25%)
  starting transfers between devices  16.3 us (15%)
  other arithmetic  15.5 us (14%)
  waiting for transfers between devices  10.6 us (10%)
  matrix products  6.39 us (6%)
  between operations  3.72 us (3%)
    all_gather x1, blocking collectives, body(): lax.all_gather(up_weight, ('lon', 'lat'), axis=0, tiled=True)  27.2 us
    ppermute x2, waiting for transfers between devices, shifted(): return lax.ppermute(block, axis, route)  9.29 us
    reshape x2, local copies, waits for them, and re-layouts, body(): grown = grown.reshape(members, levels, half_rows, half_cols, 2, 2, features)  7.43 us
    ppermute x2, starting transfers between devices, shifted(): return lax.ppermute(block, axis, route)  6.13 us
    ppermute x2, starting transfers between devices, passed_along(): return lax.ppermute(block, axis, route)  5.84 us
    reshape x1, local copies, waits for them, and re-layouts, body(): grown.transpose(0, 1, 2, 4, 3, 5, 6)  5.41 us
    reduce_sum x2, other arithmetic, normalize(): spread = jnp.mean(centred * centred, axis=-1, keepdims=True)  5.11 us
    reduce_sum x2, other arithmetic, normalize(): average = jnp.mean(values, axis=-1, keepdims=True)  4.81 us
  transfers between devices with their start and end apart: 5, of which 2 were waited for; matrix products, arithmetic and copies ran while one was open for 9% of the time, Pallas kernels for 0%

profile of v1, /device:TPU:0, one launch (start us, length us, event | category | flops | bytes accessed | tf_op | source)
XLA Modules:
  0.0 108.1 jit_solution(517471424172617197)
XLA Ops:
  0.0 1.3 %fusion.19 = (s32[1,1]{1,0:T(1,128)}, s32[1,1]{1,0:T(1,128)}) fusion(s32[1,2]{1,0:T(1,128)} %param.10), kind=kLoop, calls=%fused_computation.41 | loop fusion | bytes 16 | tf_op jit(solution)/shard_map/slice | solution.py:32
  2.7 1.6 %broadcast_select_fusion = bf16[2,8,34,6,192]{4,1,3,2,0:T(8,128)(2,1)S(1)} fusion(bf16[2,8,34,6,192]{4,1,3,2,0:T(8,128)(2,1)} %param.9, pred[34]{0:T(512)(128)(4,1)S(1)} %iota_compare_fusion.1), kind=kLoop, calls=%fused_computation.26 | loop fusion | flops 626688 | bytes 2506786 | tf_op jit(solution)/shard_map/jit(_where)/select_n | solution.py:35
  5.0 5.1 %collective-permute-start = (bf16[2,8,34,1,192]{4,1,3,2,0:T(8,128)(2,1)}, bf16[2,8,34,1,192]{4,1,3,2,0:T(8,128)(2,1)S(1)}, u32[]{:S(2)}, u32[]{:S(2)}) collective-permute-start(bf16[2,8,34,1,192]{4,1,3,2,0:T(8,128)(2,1)} %slice.29), channel_id=1, source_target_pairs={{8,0},{16,8},{24,16},{0,24},{9,1},{17,9},{25,17},{1,25},{10,2},{18... | collective-permute-start | bytes 626696 | tf_op jit(solution)/shard_map/ppermute | solution.py:10
  10.1 0.9 stack.2
  11.0 4.4 %all-to-all-start = ((bf16[16,48,384]{2,1,0:T(8,128)(2,1)}), bf16[16,48,384]{2,1,0:T(8,128)(2,1)}, u32[]{:S(2)}, u32[]{:S(2)}) async-start(bf16[16,48,384]{2,1,0:T(8,128)(2,1)} %stack.2), calls=%async_computation | async-start | bytes 1179648 | tf_op jit(solution)/shard_map/all_to_all | solution.py:55
  17.6 27.2 %all_gather.3 = bf16[384,768]{1,0:T(8,128)(2,1)} all-gather(bf16[24,768]{1,0:T(8,128)(2,1)S(1)} %copy-done.4), channel_id=1, replica_groups=mesh['lon'=4,'lat'=4,'mem'=2] {'lon','lat'}, dimensions={0}, use_global_device_ids=true | all-gather | bytes 626688 | tf_op jit(solution)/shard_map/all_gather | solution.py:66
  44.9 1.3 %collective-permute-start.1 = (bf16[2,8,1,6,192]{4,1,3,2,0:T(8,128)(2,1)S(1)}, bf16[2,8,1,6,192]{4,1,3,2,0:T(8,128)(2,1)S(1)}, u32[]{:S(2)}, u32[]{:S(2)}) collective-permute-start(bf16[2,8,1,6,192]{4,1,3,2,0:T(8,128)(2,1)S(1)} %pad_maximum_fusion), channel_id=1, source_target_pairs={{2,0},{4,2},{6,4},{3,1},{5,3},{7,5},{10,8},{12,10},{14,12},{11,9},... | collective-permute-start | bytes 110600 | tf_op jit(solution)/shard_map/ppermute | solution.py:16
  46.7 1.3 %collective-permute-done.1 = bf16[2,8,1,6,192]{4,1,3,2,0:T(8,128)(2,1)S(1)} collective-permute-done((bf16[2,8,1,6,192]{4,1,3,2,0:T(8,128)(2,1)S(1)}, bf16[2,8,1,6,192]{4,1,3,2,0:T(8,128)(2,1)S(1)}, u32[]{:S(2)}, u32[]{:S(2)}) %collective-permute-start.1) | collective-permute-done | bytes 36896 | tf_op jit(solution)/shard_map/ppermute | solution.py:16
  50.5 1.4 %copy.21 = bf16[2,8,18,3,2,2,192]{6,5,4,3,2,1,0:T(2,128)(2,1)S(1)} copy(bf16[2,8,18,3,2,2,192]{6,1,4,3,5,2,0:T(8,128)(2,1)S(1)} %fusion.7) | data formatting | bytes 2654208 | tf_op jit(solution)/shard_map/convert_element_type | solution.py:50
  51.9 2.3 %convert_element_type.32 = bf16[864,768]{1,0:T(8,128)(2,1)} reshape(bf16[2,8,18,3,2,2,192]{6,5,4,3,2,1,0:T(2,128)(2,1)S(1)} %copy.21) | data formatting | bytes 2654208 | tf_op jit(solution)/shard_map/convert_element_type | solution.py:50
  54.2 3.1 %fusion.17 = f32[864,768]{1,0:T(8,128)S(1)} fusion(bf16[384,768]{1,0:T(8,128)(2,1)S(1)} %copy-done.2, bf16[864,768]{1,0:T(8,128)(2,1)} %convert_element_type.32, bf16[768,384]{1,0:T(8,128)(2,1)} %bitcast.6), kind=kOutput, calls=%fused_computation.28 | convolution fusion | flops 1019547648 | bytes 5160960 | tf_op jit(solution)/shard_map/dot_general | solution.py:64
  57.3 4.5 %reshape.119 = f32[2,8,18,3,2,2,192]{6,5,4,3,2,1,0:T(2,128)} reshape(f32[864,768]{1,0:T(8,128)S(1)} %fusion.17) | data formatting | bytes 5308416 | tf_op jit(solution)/shard_map/reshape | solution.py:69
  61.8 4.4 %fusion.18 = f32[2,8,18,2,3,2]{5,4,3,2,1,0:T(4,128)S(1)} fusion(f32[2,8,18,3,2,2,192]{6,5,4,3,2,1,0:T(2,128)} %reshape.119), kind=kLoop, calls=%fused_computation.40 | loop fusion | flops 660096 | bytes 2668032 | tf_op jit(solution)/shard_map/reduce_sum | solution.py:20
  66.2 3.0 %copy.32 = f32[2,8,18,3,2,2,192]{6,5,3,4,2,1,0:T(2,128)} copy(f32[2,8,18,3,2,2,192]{6,5,4,3,2,1,0:T(2,128)S(1)} %copy-done.1) | data formatting | bytes 5308416 | tf_op jit(solution)/shard_map/reshape | solution.py:69
  69.5 4.4 %multiply_reduce_fusion = f32[2,8,18,2,3,2]{5,4,3,2,1,0:T(4,128)S(1)} fusion(f32[2,8,18,2,3,2]{5,4,3,2,1,0:T(4,128)S(1)} %broadcast_multiply_fusion, f32[2,8,18,3,2,2,192]{6,5,4,3,2,1,0:T(2,128)S(1)} %copy-done.1), kind=kLoop, calls=%fused_computation.12 | loop fusion | flops 1987200 | bytes 2681856 | tf_op jit(solution)/shard_map/reduce_sum | solution.py:22
  75.5 5.4 %reshape.120 = f32[3456,192]{1,0:T(8,128)} reshape(f32[2,8,18,2,3,2,192]{6,5,4,3,2,1,0:T(2,128)} %bitcast.42) | data formatting | bytes 5308416 | tf_op jit(solution)/shard_map/reshape | solution.py:70
  80.9 3.3 %convolution_convert_fusion = bf16[3456,192]{0,1:T(8,128)(2,1)S(1)} fusion(bf16[192,192]{1,0:T(8,128)(2,1)S(1)} %copy-done, f32[3456,192]{1,0:T(8,128)} %reshape.120, f32[192]{0:T(256)S(1)} %copy-done.7, f32[192]{0:T(256)S(1)} %copy-done.8, f32[3456]{0:T(1024)S(1)} %rsqrt.21, f32[3456]{0:T(1024)S(1)} %div.17), kind=kOutput, calls=%fused_computation | convolution fusion | flops 258785280 | bytes 4084224 | tf_op jit(solution)/shard_map/dot_general | solution.py:74
  84.2 2.3 %copy.23 = bf16[3456,192]{1,0:T(8,128)(2,1)} copy(bf16[3456,192]{0,1:T(8,128)(2,1)S(1)} %convolution_convert_fusion) | data formatting | bytes 2654208 | tf_op jit(solution)/shard_map/convert_element_type | solution.py:77
  86.5 2.8 %reshape.121 = bf16[2,8,36,6,192]{4,3,2,1,0:T(8,128)(2,1)S(1)} reshape(bf16[3456,192]{1,0:T(8,128)(2,1)} %copy.23) | data formatting | bytes 2654208 | tf_op jit(solution)/shard_map/reshape | solution.py:77
  89.3 4.5 %collective-permute-start.2 = (bf16[2,8,1,6,192]{4,3,2,1,0:T(8,128)(2,1)S(1)}, bf16[2,8,1,6,192]{4,3,2,1,0:T(8,128)(2,1)S(1)}, u32[]{:S(2)}, u32[]{:S(2)}) collective-permute-start(bf16[2,8,1,6,192]{4,3,2,1,0:T(8,128)(2,1)S(1)} %constant_dynamic-slice_fusion), channel_id=1, source_target_pairs={{0,2},{2,4},{4,6},{1,3},{3,5},{5,7},{8,10},{10,12},{12,14},{9,11},... | collective-permute-start | bytes 110600 | tf_op jit(solution)/shard_map/ppermute | solution.py:16
  93.9 1.9 %copy.25 = bf16[2,8,36,6,192]{4,1,3,2,0:T(8,128)(2,1)S(1)} copy(bf16[2,8,36,6,192]{4,3,2,1,0:T(8,128)(2,1)S(1)} %reshape.121) | data formatting | bytes 2654208 | tf_op jit(solution)/shard_map/reshape | solution.py:77
  96.2 1.0 collective-permute-start.3
  97.3 9.3 %collective-permute-done.3 = bf16[2,8,34,1,192]{4,1,3,2,0:T(8,128)(2,1)S(1)} collective-permute-done((bf16[2,8,34,1,192]{4,1,3,2,0:T(8,128)(2,1)S(1)}, bf16[2,8,34,1,192]{4,1,3,2,0:T(8,128)(2,1)S(1)}, u32[]{:S(2)}, u32[]{:S(2)}) %collective-permute-start.3) | collective-permute-done | bytes 208928 | tf_op jit(solution)/shard_map/ppermute | solution.py:10
  106.6 1.5 %maximum_select_fusion = bf16[2,8,34,6,192]{4,1,3,2,0:T(8,128)(2,1)} fusion(bf16[2,8,34,5,192]{4,1,3,2,0:T(8,128)(2,1)S(1)} %slice.31, bf16[2,8,34,1,192]{4,1,3,2,0:T(8,128)(2,1)S(1)} %collective-permute-done.3, pred[34]{0:T(512)(128)(4,1)S(1)} %iota_compare_fusion.1), kind=kLoop, calls=%fused_computation.25 | loop fusion | flops 1253376 | bytes 2506786 | tf_op jit(solution)/shard_map/jit(_where)/select_n | solution.py:88
  (51 shorter events, 6.2 us)
Async XLA Ops:
  0.0 80.9 %copy-start = (bf16[192,192]{1,0:T(8,128)(2,1)S(1)}, bf16[192,192]{1,0:T(8,128)(2,1)}, u32[]{:S(2)}) copy-start(bf16[192,192]{1,0:T(8,128)(2,1)} %param.17) | copy-start | bytes 221188
  2.7 7.5 %copy-start.3 = (bf16[48,384]{1,0:T(8,128)(2,1)S(1)}, bf16[48,384]{1,0:T(8,128)(2,1)}, u32[]{:S(2)}) copy-start(bf16[48,384]{1,0:T(8,128)(2,1)} %param.13) | copy-start | bytes 110596
  5.0 39.8 %collective-permute-start = (bf16[2,8,34,1,192]{4,1,3,2,0:T(8,128)(2,1)}, bf16[2,8,34,1,192]{4,1,3,2,0:T(8,128)(2,1)S(1)}, u32[]{:S(2)}, u32[]{:S(2)}) collective-permute-start(bf16[2,8,34,1,192]{4,1,3,2,0:T(8,128)(2,1)} %slice.29), channel_id=1, source_target_pairs={{8,0},{16,8},{24,16},{0,24},{9,1},{17,9},{25,17},{1,25},{10,2},{18... | collective-permute-start | bytes 626696 | tf_op jit(solution)/shard_map/ppermute | solution.py:10
  11.0 6.6 %copy-start.4 = (bf16[24,768]{1,0:T(8,128)(2,1)S(1)}, bf16[24,768]{1,0:T(8,128)(2,1)}, u32[]{:S(2)}) copy-start(bf16[24,768]{1,0:T(8,128)(2,1)} %param.14) | copy-start | bytes 110596
  11.0 43.2 %all-to-all-start = ((bf16[16,48,384]{2,1,0:T(8,128)(2,1)}), bf16[16,48,384]{2,1,0:T(8,128)(2,1)}, u32[]{:S(2)}, u32[]{:S(2)}) async-start(bf16[16,48,384]{2,1,0:T(8,128)(2,1)} %stack.2), calls=%async_computation | async-start | bytes 1179648 | tf_op jit(solution)/shard_map/all_to_all | solution.py:55
  17.6 28.9 %copy-start.5 = (f32[768]{0:T(1024)S(1)}, f32[768]{0:T(1024)}, u32[]{:S(2)}) copy-start(f32[768]{0:T(1024)} %param.11) | copy-start | bytes 9220
  17.6 29.0 %copy-start.6 = (f32[768]{0:T(1024)S(1)}, f32[768]{0:T(1024)}, u32[]{:S(2)}) copy-start(f32[768]{0:T(1024)} %param.12) | copy-start | bytes 9220
  44.9 3.1 %collective-permute-start.1 = (bf16[2,8,1,6,192]{4,1,3,2,0:T(8,128)(2,1)S(1)}, bf16[2,8,1,6,192]{4,1,3,2,0:T(8,128)(2,1)S(1)}, u32[]{:S(2)}, u32[]{:S(2)}) collective-permute-start(bf16[2,8,1,6,192]{4,1,3,2,0:T(8,128)(2,1)S(1)} %pad_maximum_fusion), channel_id=1, source_target_pairs={{2,0},{4,2},{6,4},{3,1},{5,3},{7,5},{10,8},{12,10},{14,12},{11,9},... | collective-permute-start | bytes 110600 | tf_op jit(solution)/shard_map/ppermute | solution.py:16
  51.9 2.3 %copy-start.2 = (bf16[384,768]{1,0:T(8,128)(2,1)S(1)}, bf16[384,768]{1,0:T(8,128)(2,1)}, u32[]{:S(2)}) copy-start(bf16[384,768]{1,0:T(8,128)(2,1)} %all_gather.3) | copy-start | bytes 1769476
  61.8 4.4 %copy-start.1 = (f32[2,8,18,3,2,2,192]{6,5,4,3,2,1,0:T(2,128)S(1)}, f32[2,8,18,3,2,2,192]{6,5,4,3,2,1,0:T(2,128)}, u32[]{:S(2)}) copy-start(f32[2,8,18,3,2,2,192]{6,5,4,3,2,1,0:T(2,128)} %reshape.119) | copy-start | bytes 7962628
  75.5 5.4 %copy-start.7 = (f32[192]{0:T(256)S(1)}, f32[192]{0:T(256)}, u32[]{:S(2)}) copy-start(f32[192]{0:T(256)} %param.16) | copy-start | bytes 2308
  75.5 5.4 %copy-start.8 = (f32[192]{0:T(256)S(1)}, f32[192]{0:T(256)}, u32[]{:S(2)}) copy-start(f32[192]{0:T(256)} %param.15) | copy-start | bytes 2308
  89.3 6.5 %collective-permute-start.2 = (bf16[2,8,1,6,192]{4,3,2,1,0:T(8,128)(2,1)S(1)}, bf16[2,8,1,6,192]{4,3,2,1,0:T(8,128)(2,1)S(1)}, u32[]{:S(2)}, u32[]{:S(2)}) collective-permute-start(bf16[2,8,1,6,192]{4,3,2,1,0:T(8,128)(2,1)S(1)} %constant_dynamic-slice_fusion), channel_id=1, source_target_pairs={{0,2},{2,4},{4,6},{1,3},{3,5},{5,7},{8,10},{10,12},{12,14},{9,11},... | collective-permute-start | bytes 110600 | tf_op jit(solution)/shard_map/ppermute | solution.py:16
  96.2 10.4 %collective-permute-start.3 = (bf16[2,8,34,1,192]{4,1,3,2,0:T(8,128)(2,1)S(1)}, bf16[2,8,34,1,192]{4,1,3,2,0:T(8,128)(2,1)S(1)}, u32[]{:S(2)}, u32[]{:S(2)}) collective-permute-start(bf16[2,8,34,1,192]{4,1,3,2,0:T(8,128)(2,1)S(1)} %slice.30), channel_id=1, source_target_pairs={{24,0},{0,8},{8,16},{16,24},{25,1},{1,9},{9,17},{17,25},{26,2},{2,... | collective-permute-start | bytes 626696 | tf_op jit(solution)/shard_map/ppermute | solution.py:10
